TPU v7x, 32 devices: a whole 2x2x4 slice. The times are simulated.
32 devices in a mesh: rep: 4 (over x, core), grp: 8 (over z, y).
Axes of the slice: x: 2, y: 2, z: 4, core: 2. Of those that a mesh axis runs over, the one named last changes fastest.
Arguments:
- tokens: bfloat16 [8192, 2304], P(('rep', 'grp')), may hold values from -6 to 6
- norm_gain: float32 [2304], replicated, may hold values from 0.25 to 1.75
- key_weight: bfloat16 [2304, 1024], P('grp'), may hold values from -0.125 to 0.125
- key_grad: bfloat16 [8192, 1024], P(('rep', 'grp')), may hold values from -6 to 6
Outputs:
- token_grad: bfloat16 [8192, 2304], P(('rep', 'grp'))
- weight_grad: float32 [2304, 1024], P('grp', 'rep')
- gain_grad: float32 [2304], replicated
All inputs are finite; a program needn't handle non-finite values.
Results may differ from a plain program's by a relative error of at most 0.023.
Values may be sent and summed in bfloat16 or wider, within the bound.
A program may use at most 64 MiB of HBM per device.

v0:
```python
import jax
import jax.numpy as jnp
from jax import lax
from jax.sharding import PartitionSpec as P

epsilon = 1e-06


def shards(tokens, norm_gain, key_weight, key_grad):
    total_tokens = tokens.shape[0] * lax.axis_size("rep") * lax.axis_size("grp")
    grad_scale = total_tokens ** (-0.5)
    wide_tokens = tokens.astype(jnp.float32)
    inv_rms = lax.rsqrt(jnp.mean(wide_tokens * wide_tokens, axis=1, keepdims=True) + epsilon)
    normed = (wide_tokens * inv_rms * norm_gain).astype(jnp.bfloat16)
    partial_value = lax.dot_general(
        normed, key_grad, (((0,), (0,)), ((), ())), preferred_element_type=jnp.float32
    )
    d_normed = lax.dot_general(
        key_grad,
        lax.all_gather(key_weight, "grp", axis=0, tiled=True),
        (((1,), (1,)), ((), ())),
        preferred_element_type=jnp.float32,
    )
    section_one = lax.psum_scatter(
        partial_value.astype(jnp.bfloat16), "rep", scatter_dimension=1, tiled=True
    ).astype(jnp.float32)
    weight_sum = lax.psum_scatter(section_one, "grp", scatter_dimension=0, tiled=True)
    gain_local = jnp.sum(d_normed * wide_tokens * inv_rms, axis=0)
    gain_total = lax.psum(gain_local, ("rep", "grp"))
    scaled = d_normed * norm_gain
    inner_mean = jnp.mean(scaled * wide_tokens, axis=1, keepdims=True)
    token_grad = (inv_rms * (scaled - wide_tokens * inv_rms * inv_rms * inner_mean)).astype(
        jnp.bfloat16
    )
    return (token_grad, weight_sum * grad_scale, gain_total * grad_scale)


def solution(mesh):
    in_specs = (P(("rep", "grp"), None), P(), P("grp", None), P(("rep", "grp"), None))
    out_specs = (P(("rep", "grp"), None), P("grp", "rep"), P())
    return jax.shard_map(shards, mesh=mesh, in_specs=in_specs, out_specs=out_specs, check_vma=False)
```

profile of v0, /device:TPU:0, one launch (start us, length us, event | category | flops | bytes accessed | tf_op | source)
XLA Modules:
  0.0 180.5 jit_solution(7372656190298099384)
XLA Ops:
  8.0 0.0 copy-start
  8.0 0.0 reduce-scatter.3.cloned.1.call-start
  8.1 1.6 fusion.7
  9.7 0.0 copy-done
  9.7 5.0 %convolution_convert_fusion = bf16[2304,1024]{1,0:T(8,128)(2,1)} fusion(bf16[256,1024]{1,0:T(8,128)(2,1)S(1)} %copy-done, bf16[256,2304]{1,0:T(8,128)(2,1)} %param.4, f32[2304]{0:T(1024)} %param.5, f32[256]{0:T(256)S(1)} %add_rsqrt_fusion), kind=kOutput, calls=%fused_computation | convolution fusion | flops 1212678144 | bytes 6432768 | tf_op jit(solution)/shard_map/dot_general | solution.py:15
  14.7 0.0 reduce-scatter.3.cloned.1.call-update
  14.7 0.0 all-gather.2.cloned.1.call-start
  14.8 0.5 all-gather.2.cloned.1.call-update
  15.3 0.0 copy-start.1
  15.3 0.0 copy-start.2
  15.3 0.0 reduce-scatter.5.cloned.1.call-start
  15.4 50.0 %reduce-scatter.3.cloned.1.call-done = bf16[2304,256]{1,0:T(8,128)(2,1)} async-done(((bf16[2304,1024]{1,0:T(8,128)(2,1)}), bf16[2304,256]{1,0:T(8,128)(2,1)}) %reduce-scatter.3.cloned.1.call-update) | async-done | bytes 1179664 | tf_op jit(solution)/shard_map/reduce_scatter | solution.py:24
  65.3 2.9 %convert_element_type.19 = f32[2304,256]{1,0:T(8,128)} convert(bf16[2304,256]{1,0:T(8,128)(2,1)} %reduce-scatter.3.cloned.1.call-done) | non-fusion elementwise | flops 589824 | bytes 3538944 | tf_op jit(solution)/shard_map/convert_element_type | solution.py:26
  68.3 0.0 reduce-scatter.5.cloned.1.call-update
  68.3 30.9 %all-gather.2.cloned.1.call-done = bf16[2304,1024]{1,0:T(8,128)(2,1)} async-done(((bf16[288,1024]{1,0:T(8,128)(2,1)}), bf16[2304,1024]{1,0:T(8,128)(2,1)}) %all-gather.2.cloned.1.call-update) | async-done | bytes 4718608 | tf_op jit(solution)/shard_map/all_gather | solution.py:20
  99.2 0.0 copy-done.1
  99.2 0.0 copy-done.2
  99.2 5.6 %fusion.10 = (f32[2304]{0:T(1024)S(1)}, f32[256]{0:T(256)S(1)}, f32[256,2304]{1,0:T(8,128)}) fusion(bf16[256,2304]{1,0:T(8,128)(2,1)S(1)} %copy-done.1, f32[256]{0:T(256)S(1)} %add_rsqrt_fusion, f32[2304]{0:T(1024)S(1)} %copy-done.2, bf16[256,1024]{1,0:T(8,128)(2,1)S(1)} %copy-done, bf16[2304,1024]{1,0:T(8,128)(2,1)} %all-gather.2.cloned.1.call-done), kind=kOutput, calls=%fused_computation.15 | convolution fusion | flops 1212085760 | bytes 8802304 | tf_op jit(solution)/shard_map/dot_general | solution.py:18
  104.8 39.4 %psum.7 = f32[2304]{0:T(1024)S(1)} all-reduce(f32[2304]{0:T(1024)S(1)} %get-tuple-element.3), channel_id=1, replica_groups=mesh['rep'=4,'grp'=8] {'rep','grp'}, use_global_device_ids=true, to_apply=%region_5.0 | all-reduce | flops 2304 | bytes 18432 | tf_op jit(solution)/shard_map/psum | solution.py:29
  144.2 0.6 broadcast_multiply_fusion.1
  144.8 3.4 %fusion.5 = bf16[256,2304]{1,0:T(8,128)(2,1)} fusion(bf16[256,2304]{1,0:T(8,128)(2,1)S(1)} %copy-done.1, f32[256,2304]{1,0:T(8,128)} %get-tuple-element.5, f32[256]{0:T(256)S(1)} %broadcast_multiply_fusion.2, f32[2304]{0:T(1024)S(1)} %copy-done.2, f32[256]{0:T(256)S(1)} %add_rsqrt_fusion), kind=kLoop, calls=%fused_computation.10 | loop fusion | flops 4718592 | bytes 4729856 | tf_op jit(solution)/shard_map/convert_element_type | solution.py:32
  148.2 23.2 %reduce-scatter.5.cloned.1.call-done = f32[288,256]{1,0:T(8,128)} async-done(((f32[2304,256]{1,0:T(8,128)}), f32[288,256]{1,0:T(8,128)}) %reduce-scatter.5.cloned.1.call-update) | async-done | bytes 294928 | tf_op jit(solution)/shard_map/reduce_scatter | solution.py:27
  171.4 1.7 broadcast_multiply_fusion
  (2 shorter events, 0.0 us)
Async XLA Ops:
  8.0 1.7 copy-start
  8.0 57.3 %reduce-scatter.3.cloned.1.call-start = ((), (), s32[]{:S(2)}) async-start(), calls=%async_computation.3 | async-start | bytes 5898240 | tf_op jit(solution)/shard_map/reduce_scatter | solution.py:24
  14.7 84.5 %all-gather.2.cloned.1.call-start = ((), (), s32[]{:S(2)}) async-start(), calls=%async_computation.2 | async-start | bytes 5308416 | tf_op jit(solution)/shard_map/all_gather | solution.py:20
  15.3 83.9 %copy-start.1 = (bf16[256,2304]{1,0:T(8,128)(2,1)S(1)}, bf16[256,2304]{1,0:T(8,128)(2,1)}, u32[]{:S(2)}) copy-start(bf16[256,2304]{1,0:T(8,128)(2,1)} %param.4) | copy-start | bytes 3538948
  15.3 83.9 %copy-start.2 = (f32[2304]{0:T(1024)S(1)}, f32[2304]{0:T(1024)}, u32[]{:S(2)}) copy-start(f32[2304]{0:T(1024)} %param.5) | copy-start | bytes 27652
  15.3 156.1 %reduce-scatter.5.cloned.1.call-start = ((), (), s32[]{:S(2)}) async-start(), calls=%async_computation.4 | async-start | bytes 2654208 | tf_op jit(solution)/shard_map/reduce_scatter | solution.py:27
Sparse Core Ops, SparseCore 0:
  14.8 50.4 reduce-scatter.2
Sparse Core Ops, SparseCore 1:
  17.4 81.8 all-gather.1
  102.6 68.8 reduce-scatter.4
where the time goes:
time: 181 us
  waiting for transfers between devices  105 us (58%)
  blocking collectives  39.4 us (22%)
  between operations  15.5 us (9%)
  matrix products  10.6 us (6%)
  other arithmetic  10.2 us (6%)
    reduce_scatter x1, waiting for transfers between devices, shards(): lax.psum_scatter(partial_value.astype(jnp.bfloat16), 'rep', scatter_dimen...  50 us
    psum x1, blocking collectives, shards(): gain_total = lax.psum(gain_local, ('rep', 'grp'))  39.4 us
    all_gather x1, waiting for transfers between devices, shards(): lax.all_gather(key_weight, 'grp', axis=0, tiled=True)  30.9 us
    reduce_scatter x1, waiting for transfers between devices, shards(): lax.psum_scatter(section_one, 'grp', scatter_dimension=0, tiled=True)  23.2 us
    dot_general x1, matrix products, shards(): lax.dot_general(key_grad, lax.all_gather(key_weight, 'grp', axis=0, tiled...  5.59 us
    dot_general x1, matrix products, shards(): lax.dot_general(normed, key_grad, (((0,), (0,)), ((), ())), preferred_ele...  4.97 us
  transfers between devices with their start and end apart: 3, of which 3 were waited for; matrix products, arithmetic and copies ran while one was open for 7% of the time, Pallas kernels for 0%

commit v1 on v0

--- a/solution.py
+++ b/solution.py
@@ -1,12 +1,285 @@
+import functools
+
 import jax
 import jax.numpy as jnp
 from jax import lax
+from jax.experimental import pallas as pl
+from jax.experimental.pallas import tpu as pltpu
 from jax.sharding import PartitionSpec as P
 
 epsilon = 1e-06
-
-
-def shards(tokens, norm_gain, key_weight, key_grad):
+MESH = pl.DeviceIdType.MESH
+LANES = 128
+
+
+def flip(i, bits):
+    bit = 1
+    while bit <= bits:
+        if bits & bit:
+            i = i + bit * (1 - 2 * lax.rem(lax.div(i, bit), 2))
+        bit *= 2
+    return i
+
+
+def kernel(
+    n_z, grad_scale,
+    tok_ref, gain_ref, w_ref, kg_ref,
+    tg_ref, wg_ref, gg_ref,
+    wfull, normed_t, dn, mine, give, take, in1, in2, in3, gsend, grecv,
+    w_send, w_recv, c_send, c_recv, s1_send, s1_recv, s2_send, s2_recv, s3_send, s3_recv, g_send, g_recv,
+):
+    rep, grp = lax.axis_index("rep"), lax.axis_index("grp")
+    x, c = lax.div(rep, 2), lax.rem(rep, 2)
+    z, y = lax.div(grp, 2), lax.rem(grp, 2)
+    rows, keys = w_ref.shape
+    features = tok_ref.shape[1]
+    cols = mine.shape[-1]
+    peer_c = (2 * x + 1 - c, grp)
+    peer_x = (2 * (1 - x) + c, grp)
+    peer_y = (rep, 2 * z + 1 - y)
+    peer_z = [None] + [(rep, 2 * flip(z, k) + y) for k in range(1, n_z)]
+
+    barrier = pltpu.get_barrier_semaphore()
+    peers = [peer_c, peer_x, peer_y] + peer_z[1:]
+    for peer in peers:
+        pl.semaphore_signal(barrier, inc=1, device_id=peer, device_id_type=MESH)
+    pl.semaphore_wait(barrier, len(peers))
+
+    sends = []
+
+    def send(src, dst, s_sem, r_sem, peer):
+        copy = pltpu.make_async_remote_copy(
+            src_ref=src, dst_ref=dst, send_sem=s_sem, recv_sem=r_sem, device_id=peer, device_id_type=MESH
+        )
+        copy.start()
+        sends.append(copy)
+
+    def arrived(dst, sem):
+        pltpu.make_async_remote_copy(
+            src_ref=dst, dst_ref=dst, send_sem=sem, recv_sem=sem, device_id=peer_c, device_id_type=MESH
+        ).wait_recv()
+
+    def row_at(k, yy):
+        g = 2 * flip(z, k) + (1 - y if yy else y)
+        return pl.ds(pl.multiple_of(g * rows, 16), rows)
+
+    def col_at(xx, cc):
+        r = 2 * (1 - x if xx else x) + (1 - c if cc else c)
+        return pl.ds(pl.multiple_of(r * cols, LANES), cols)
+
+    def piece(xx, cc, k, yy):
+        return wfull.at[row_at(k, yy), col_at(xx, cc)]
+
+    def got(xx, cc, k, yy):
+        arrived(piece(xx, cc, k, yy), w_recv.at[xx, cc, k, yy])
+
+    def w_fwd(axis, xx, k, yy):
+        there = {0: (xx, 1, k, yy), 1: (1 - xx, 0, k, yy), 2: (xx, 0, k, 1 - yy)}[axis]
+        peer = (peer_c, peer_x, peer_y)[axis]
+        ref = piece(xx, 0, k, yy)
+        send(ref, ref, w_send.at[axis, xx, k, yy], w_recv.at[there], peer)
+
+    own_cols = w_ref.at[:, col_at(0, 0)]
+    for k in range(1, n_z):
+        send(own_cols, piece(0, 0, 0, 0), w_send.at[3, 0, k, 0], w_recv.at[0, 0, k, 0], peer_z[k])
+    send(own_cols, piece(0, 0, 0, 0), w_send.at[2, 0, 0, 0], w_recv.at[0, 0, 0, 1], peer_y)
+
+    acc = None
+    for j in range(features // LANES):
+        t = tok_ref[:, j * LANES:(j + 1) * LANES].astype(jnp.float32)
+        acc = t * t if acc is None else acc + t * t
+    inv = lax.rsqrt(jnp.sum(acc, axis=1, keepdims=True) / features + epsilon)
+    for j in range(features // LANES):
+        at = slice(j * LANES, (j + 1) * LANES)
+        t = tok_ref[:, at].astype(jnp.float32)
+        normed_t[at, :] = (t * inv * gain_ref[:, at]).T.astype(jnp.bfloat16)
+
+    def partial(k):
+        for cc in (1, 0):
+            for yy in (0, 1):
+                for xx in (0, 1):
+                    block = jnp.dot(
+                        normed_t[row_at(k, yy), :], kg_ref[:, col_at(xx, cc)], preferred_element_type=jnp.float32
+                    ).astype(jnp.bfloat16)
+                    (give if cc else mine)[k, yy, xx] = block
+            if cc:
+                send(give.at[k], take.at[k], c_send.at[k], c_recv.at[k], peer_c)
+
+    def add(k, yy, xx, ref):
+        mine[k, yy, xx] = (
+            mine[k, yy, xx].astype(jnp.float32) + ref[...].astype(jnp.float32)
+        ).astype(jnp.bfloat16)
+
+    def x_first(k):
+        return k % 2 == 1
+
+    def stage1(k):
+        arrived(take.at[k], c_recv.at[k])
+        order = [(0, 1), (1, 1), (0, 0), (1, 0)] if x_first(k) else [(1, 0), (1, 1), (0, 0), (0, 1)]
+        for n, (yy, xx) in enumerate(order):
+            add(k, yy, xx, take.at[k, yy, xx])
+            if n < 2:
+                slot = yy if x_first(k) else xx
+                send(
+                    mine.at[k, yy, xx], in1.at[k, slot], s1_send.at[k, slot], s1_recv.at[k, slot],
+                    peer_x if x_first(k) else peer_y,
+                )
+
+    def stage2(k):
+        for slot in (1, 0):
+            arrived(in1.at[k, slot], s1_recv.at[k, slot])
+            yy, xx = (slot, 0) if x_first(k) else (0, slot)
+            add(k, yy, xx, in1.at[k, slot])
+            if slot:
+                send(mine.at[k, yy, xx], in2.at[k], s2_send.at[k], s2_recv.at[k], peer_y if x_first(k) else peer_x)
+
+    def stage3(k):
+        arrived(in2.at[k], s2_recv.at[k])
+        add(k, 0, 0, in2.at[k])
+        send(mine.at[k, 0, 0], in3.at[k], s3_send.at[k], s3_recv.at[k], peer_z[k])
+
+    def from_z(k):
+        got(0, 0, k, 0)
+        for axis in (1, 2, 0):
+            w_fwd(axis, 0, k, 0)
+
+    def diag_by_x(k):
+        return k == 0 or k == n_z - 1
+
+    def from_x(k):
+        got(1, 0, k, 0)
+        if not diag_by_x(k):
+            w_fwd(2, 1, k, 0)
+        w_fwd(0, 1, k, 0)
+
+    def from_y(k):
+        got(0, 0, k, 1)
+        if diag_by_x(k):
+            w_fwd(1, 0, k, 1)
+        w_fwd(0, 0, k, 1)
+
+    wfull[row_at(0, 0), :] = w_ref[...]
+    far = list(range(n_z - 1, -1, -1))
+    near = list(range(1, n_z))
+    partial(far[0])
+    from_y(0)
+    for n, k in enumerate(near):
+        partial(far[n + 1])
+        from_z(k)
+        stage1(far[n])
+    stage1(far[-1])
+    for n, k in enumerate(near):
+        from_x(k)
+        from_y(k)
+        stage2(far[n])
+    stage2(far[-1])
+    for k in range(n_z):
+        got(1, 0, k, 1)
+        w_fwd(0, 1, k, 1)
+    for k in far[:-1]:
+        stage3(k)
+    for k in range(n_z):
+        for yy in (0, 1):
+            for xx in (0, 1):
+                if k or yy:
+                    got(xx, 1, k, yy)
+
+    wide = 2 * LANES
+    inner = jnp.zeros((tok_ref.shape[0], LANES), jnp.float32)
+    for j in range(features // wide):
+        at = slice(j * wide, (j + 1) * wide)
+        d = lax.dot_general(
+            kg_ref[...], wfull[at, :], (((1,), (1,)), ((), ())), preferred_element_type=jnp.float32
+        )
+        dn[:, at] = d
+        dt = d * tok_ref[:, at].astype(jnp.float32)
+        gsend[0, :, at] = jnp.sum(dt * inv, axis=0, keepdims=True)
+        scaled = dt * gain_ref[:, at]
+        inner = inner + scaled[:, :LANES] + scaled[:, LANES:]
+    send(gsend.at[0], grecv.at[0], g_send.at[0], g_recv.at[0], peer_c)
+    mean = jnp.sum(inner, axis=1, keepdims=True) / features
+    pull = inv * inv * mean
+
+    def token_grad(lo, hi):
+        for j in range(lo, hi):
+            at = slice(j * wide, (j + 1) * wide)
+            t = tok_ref[:, at].astype(jnp.float32)
+            tg_ref[:, at] = (inv * (dn[:, at] * gain_ref[:, at] - t * pull)).astype(jnp.bfloat16)
+
+    steps = features // wide
+    cuts = [steps * n // 3 for n in range(4)]
+    for n, peer in enumerate((peer_x, peer_y, None)):
+        token_grad(cuts[n], cuts[n + 1])
+        arrived(grecv.at[n], g_recv.at[n])
+        gsend[n + 1] = gsend[n] + grecv[n]
+        if peer is not None:
+            send(gsend.at[n + 1], grecv.at[n + 1], g_send.at[n + 1], g_recv.at[n + 1], peer)
+        else:
+            for k in range(1, n_z):
+                send(gsend.at[n + 1], grecv.at[2 + k], g_send.at[2 + k], g_recv.at[2 + k], peer_z[k])
+
+    arrived(in2.at[0], s2_recv.at[0])
+    total = mine[0, 0, 0].astype(jnp.float32) + in2[0].astype(jnp.float32)
+    for k in range(1, n_z):
+        arrived(in3.at[k], s3_recv.at[k])
+        total = total + in3[k].astype(jnp.float32)
+    wg_ref[...] = total * grad_scale
+
+    terms = [gsend[3]]
+    for k in range(1, n_z):
+        arrived(grecv.at[2 + k], g_recv.at[2 + k])
+        terms.append(grecv[2 + k])
+    while len(terms) > 1:
+        terms = [terms[i] + terms[i + 1] for i in range(0, len(terms), 2)]
+    gg_ref[...] = terms[0] * grad_scale
+    for copy in sends:
+        copy.wait_send()
+
+
+def fused(n_rep, n_grp, tokens, norm_gain, key_weight, key_grad):
+    n_tok, features = tokens.shape
+    rows, keys = key_weight.shape
+    cols, n_z = keys // n_rep, n_grp // 2
+    grad_scale = (n_tok * n_rep * n_grp) ** (-0.5)
+    vmem = pl.BlockSpec(memory_space=pltpu.VMEM)
+    bf16, f32, dma = jnp.bfloat16, jnp.float32, pltpu.SemaphoreType.DMA
+    block = (rows, cols)
+    token_grad, weight_grad, gain_grad = pl.pallas_call(
+        functools.partial(kernel, n_z, grad_scale),
+        out_shape=(
+            jax.ShapeDtypeStruct((n_tok, features), bf16),
+            jax.ShapeDtypeStruct(block, f32),
+            jax.ShapeDtypeStruct((1, features), f32),
+        ),
+        in_specs=[vmem] * 4,
+        out_specs=(vmem,) * 3,
+        scratch_shapes=[
+            pltpu.VMEM((features, keys), bf16),
+            pltpu.VMEM((features, n_tok), bf16),
+            pltpu.VMEM((n_tok, features), f32),
+            pltpu.VMEM((n_z, 2, 2) + block, bf16),
+            pltpu.VMEM((n_z, 2, 2) + block, bf16),
+            pltpu.VMEM((n_z, 2, 2) + block, bf16),
+            pltpu.VMEM((n_z, 2) + block, bf16),
+            pltpu.VMEM((n_z,) + block, bf16),
+            pltpu.VMEM((n_z,) + block, bf16),
+            pltpu.VMEM((4, 1, features), f32),
+            pltpu.VMEM((n_z + 2, 1, features), f32),
+            dma((4, 2, n_z, 2)), dma((2, 2, n_z, 2)),
+            dma((n_z,)), dma((n_z,)),
+            dma((n_z, 2)), dma((n_z, 2)),
+            dma((n_z,)), dma((n_z,)),
+            dma((n_z,)), dma((n_z,)),
+            dma((n_z + 2,)), dma((n_z + 2,)),
+        ],
+        compiler_params=pltpu.CompilerParams(
+            collective_id=0, has_side_effects=True, vmem_limit_bytes=48 * 1024 * 1024
+        ),
+    )(tokens, norm_gain.reshape(1, features), key_weight, key_grad)
+    return token_grad, weight_grad, gain_grad.reshape(features)
+
+
+def plain(tokens, norm_gain, key_weight, key_grad):
     total_tokens = tokens.shape[0] * lax.axis_size("rep") * lax.axis_size("grp")
     grad_scale = total_tokens ** (-0.5)
     wide_tokens = tokens.astype(jnp.float32)
@@ -35,6 +308,18 @@
     return (token_grad, weight_sum * grad_scale, gain_total * grad_scale)
 
 
+def shards(tokens, norm_gain, key_weight, key_grad):
+    n_rep, n_grp = lax.axis_size("rep"), lax.axis_size("grp")
+    n_z = n_grp // 2
+    if (
+        n_rep == 2 * 2 and n_grp % 2 == 0 and n_z & (n_z - 1) == 0 and 1 < n_z <= 4
+        and key_weight.shape[1] % (n_rep * LANES) == 0 and key_weight.shape[0] % 16 == 0
+        and tokens.shape[1] % (2 * LANES) == 0 and tokens.shape[0] % LANES == 0
+    ):
+        return fused(n_rep, n_grp, tokens, norm_gain, key_weight, key_grad)
+    return plain(tokens, norm_gain, key_weight, key_grad)
+
+
 def solution(mesh):
     in_specs = (P(("rep", "grp"), None), P(), P("grp", None), P(("rep", "grp"), None))
     out_specs = (P(("rep", "grp"), None), P("grp", "rep"), P())

time: 181 us -> 68 us (0.38)
  waiting for transfers between devices: 105 us -> 0 us
  Pallas kernels: 0 us -> 60.6 us
  blocking collectives: 39.4 us -> 0 us
  between operations: 15.5 us -> 0.65 us
  matrix products: 10.6 us -> 0 us
  other arithmetic: 10.2 us -> 0.63 us
  local copies, waits for them, and re-layouts: 0.02 us -> 5.81 us
    reduce_scatter x2 -> x0, waiting for transfers between devices: 73.2 us -> none  [the longest x1 50 us: shards(): lax.psum_scatter(partial_value.astype(jnp.bfloat16), 'rep', scatter_dimen...]
    pallas_call x0 -> x1, Pallas kernels: none -> 60.6 us  [fused(): pl.pallas_call(functools.partial(kernel, n_z, grad_scale), out_shape=(jax...]
    psum x1 -> x0, blocking collectives: 39.4 us -> none  [shards(): gain_total = lax.psum(gain_local, ('rep', 'grp'))]
    all_gather x1 -> x0, waiting for transfers between devices: 30.9 us -> none  [shards(): lax.all_gather(key_weight, 'grp', axis=0, tiled=True)]
    dot_general x2 -> x0, matrix products: 10.6 us -> none  [the longest x1 5.59 us: shards(): lax.dot_general(key_grad, lax.all_gather(key_weight, 'grp', axis=0, tiled...]
    convert_element_type x2 -> x0, other arithmetic: 6.26 us -> none  [the longest x1 3.36 us: shards(): (inv_rms * (scaled - wide_tokens * inv_rms * inv_rms * inner_mean)).astyp...]
    unnamed x6 -> x8, local copies, waits for them, and re-layouts: 0.02 us -> 5.1 us
    mul x2 -> x0, other arithmetic: 2.3 us -> none  [shards(): return (token_grad, weight_sum * grad_scale, gain_total * grad_scale)]
  transfers between devices with their start and end apart: 3 -> 0, of which waited for: 3 -> 0; matrix products, arithmetic and copies ran while one was open for 7% -> 0% of each run, Pallas kernels for 0% -> 0%
where the time goes in v1:
time: 68 us; the launch traced here: 67.7 us
  Pallas kernels  60.6 us (89%)
  local copies, waits for them, and re-layouts  5.81 us (9%)
    pallas_call x1, Pallas kernels, fused(): pl.pallas_call(functools.partial(kernel, n_z, grad_scale), out_shape=(jax...  60.6 us
    unnamed x8, local copies, waits for them, and re-layouts  5.1 us

profile of v1, /device:TPU:0, one launch (start us, length us, event | category | flops | bytes accessed | tf_op | source)
XLA Modules:
  0.0 67.7 jit_solution(2777389590619808038)
XLA Ops:
  0.6 0.7 %reshape.12.gain_ref = f32[1,2304]{1,0:T(1,128)S(1)} reshape(f32[2304]{0:T(1024)} %param.5) | data formatting | bytes 18432 | tf_op jit(solution)/shard_map/reshape | solution.py:278
  1.3 0.0 copy-start
  1.3 1.3 %copy-done = bf16[256,2304]{1,0:T(8,128)(2,1)S(1)} copy-done((bf16[256,2304]{1,0:T(8,128)(2,1)S(1)}, bf16[256,2304]{1,0:T(8,128)(2,1)}, u32[]{:S(2)}) %copy-start) | copy-done | bytes 1179672
  2.6 0.0 copy-start.1
  2.6 1.1 %copy-done.1 = bf16[288,1024]{1,0:T(8,128)(2,1)S(1)} copy-done((bf16[288,1024]{1,0:T(8,128)(2,1)S(1)}, bf16[288,1024]{1,0:T(8,128)(2,1)}, u32[]{:S(2)}) %copy-start.1) | copy-done | bytes 589848
  3.7 0.0 copy-start.2
  3.7 1.0 %copy-done.2 = bf16[256,1024]{1,0:T(8,128)(2,1)S(1)} copy-done((bf16[256,1024]{1,0:T(8,128)(2,1)S(1)}, bf16[256,1024]{1,0:T(8,128)(2,1)}, u32[]{:S(2)}) %copy-start.2) | copy-done | bytes 524312
  4.7 60.6 %shard_map.67 = (bf16[256,2304]{1,0:T(8,128)(2,1)S(1)}, f32[288,256]{1,0:T(8,128)S(1)}, f32[1,2304]{1,0:T(1,128)S(1)}) custom-call(bf16[256,2304]{1,0:T(8,128)(2,1)S(1)} %copy-done, f32[1,2304]{1,0:T(1,128)S(1)} %reshape.12.gain_ref, bf16[288,1024]{1,0:T(8,128)(2,1)S(1)} %copy-done.1, bf16[256,1024]{1,0:T(8,128)(2,1)S(1)} %copy-done.2), custom_call_target="tpu_custom_call" | custom-call | tf_op jit(solution)/shard_map/pallas_call | solution.py:247
  65.3 0.6 reduce
  65.9 1.0 %copy.9 = bf16[256,2304]{1,0:T(8,128)(2,1)} copy(bf16[256,2304]{1,0:T(8,128)(2,1)S(1)} %get-tuple-element.12) | data formatting | bytes 2359296
  67.0 0.7 %copy.10 = f32[288,256]{1,0:T(8,128)} copy(f32[288,256]{1,0:T(8,128)S(1)} %get-tuple-element.13) | data formatting | bytes 589824
Async XLA Ops:
  1.3 1.3 %copy-start = (bf16[256,2304]{1,0:T(8,128)(2,1)S(1)}, bf16[256,2304]{1,0:T(8,128)(2,1)}, u32[]{:S(2)}) copy-start(bf16[256,2304]{1,0:T(8,128)(2,1)} %tok_ref.1) | copy-start | bytes 3538948
  2.6 1.1 %copy-start.1 = (bf16[288,1024]{1,0:T(8,128)(2,1)S(1)}, bf16[288,1024]{1,0:T(8,128)(2,1)}, u32[]{:S(2)}) copy-start(bf16[288,1024]{1,0:T(8,128)(2,1)} %w_ref.1) | copy-start | bytes 1769476
  3.7 1.0 %copy-start.2 = (bf16[256,1024]{1,0:T(8,128)(2,1)S(1)}, bf16[256,1024]{1,0:T(8,128)(2,1)}, u32[]{:S(2)}) copy-start(bf16[256,1024]{1,0:T(8,128)(2,1)} %kg_ref.1) | copy-start | bytes 1572868

commit v2 on v1

--- a/solution.py
+++ b/solution.py
@@ -23,9 +23,9 @@
 
 def kernel(
     n_z, grad_scale,
-    tok_ref, gain_ref, w_ref, kg_ref,
+    tok_hbm, gain_hbm, w_ref, kg_hbm,
     tg_ref, wg_ref, gg_ref,
-    wfull, normed_t, dn, mine, give, take, in1, in2, in3, gsend, grecv,
+    tok_ref, gain_ref, kg_ref, load_sem, wfull, normed_t, dn, mine, give, take, in1, in2, in3, gsend, grecv,
     w_send, w_recv, c_send, c_recv, s1_send, s1_recv, s2_send, s2_recv, s3_send, s3_recv, g_send, g_recv,
 ):
     rep, grp = lax.axis_index("rep"), lax.axis_index("grp")
@@ -39,6 +39,19 @@
     peer_y = (rep, 2 * z + 1 - y)
     peer_z = [None] + [(rep, 2 * flip(z, k) + y) for k in range(1, n_z)]
 
+    def row_at(k, yy):
+        g = 2 * flip(z, k) + (1 - y if yy else y)
+        return pl.ds(pl.multiple_of(g * rows, 16), rows)
+
+    loads = [
+        pltpu.make_async_copy(src, dst, load_sem.at[n])
+        for n, (src, dst) in enumerate(
+            ((tok_hbm, tok_ref), (gain_hbm, gain_ref), (kg_hbm, kg_ref), (w_ref, wfull.at[row_at(0, 0), :]))
+        )
+    ]
+    for load in loads:
+        load.start()
+
     barrier = pltpu.get_barrier_semaphore()
     peers = [peer_c, peer_x, peer_y] + peer_z[1:]
     for peer in peers:
@@ -59,10 +72,6 @@
             src_ref=dst, dst_ref=dst, send_sem=sem, recv_sem=sem, device_id=peer_c, device_id_type=MESH
         ).wait_recv()
 
-    def row_at(k, yy):
-        g = 2 * flip(z, k) + (1 - y if yy else y)
-        return pl.ds(pl.multiple_of(g * rows, 16), rows)
-
     def col_at(xx, cc):
         r = 2 * (1 - x if xx else x) + (1 - c if cc else c)
         return pl.ds(pl.multiple_of(r * cols, LANES), cols)
@@ -79,20 +88,30 @@
         ref = piece(xx, 0, k, yy)
         send(ref, ref, w_send.at[axis, xx, k, yy], w_recv.at[there], peer)
 
-    own_cols = w_ref.at[:, col_at(0, 0)]
+    def own_to(axis, xx, k, peer):
+        there = (xx, 0, 0, 1) if axis == 2 else (xx, 0, k, 0)
+        send(
+            w_ref.at[:, col_at(xx, 0)], piece(xx, 0, 0, 0), w_send.at[axis, xx, k, 0], w_recv.at[there], peer
+        )
+
+    own_to(2, 0, 0, peer_y)
     for k in range(1, n_z):
-        send(own_cols, piece(0, 0, 0, 0), w_send.at[3, 0, k, 0], w_recv.at[0, 0, k, 0], peer_z[k])
-    send(own_cols, piece(0, 0, 0, 0), w_send.at[2, 0, 0, 0], w_recv.at[0, 0, 0, 1], peer_y)
-
+        own_to(3, 0, k, peer_z[k])
+    own_to(2, 1, 0, peer_y)
+    for k in range(1, n_z - 1):
+        own_to(3, 1, k, peer_z[k])
+
+    loads[0].wait()
     acc = None
     for j in range(features // LANES):
         t = tok_ref[:, j * LANES:(j + 1) * LANES].astype(jnp.float32)
         acc = t * t if acc is None else acc + t * t
     inv = lax.rsqrt(jnp.sum(acc, axis=1, keepdims=True) / features + epsilon)
+    loads[1].wait()
     for j in range(features // LANES):
         at = slice(j * LANES, (j + 1) * LANES)
         t = tok_ref[:, at].astype(jnp.float32)
-        normed_t[at, :] = (t * inv * gain_ref[:, at]).T.astype(jnp.bfloat16)
+        normed_t[at, :] = (t * inv * gain_ref[at].reshape(1, -1)).T.astype(jnp.bfloat16)
 
     def partial(k):
         for cc in (1, 0):
@@ -113,71 +132,76 @@
     def x_first(k):
         return k % 2 == 1
 
-    def stage1(k):
+    def core_in(k):
         arrived(take.at[k], c_recv.at[k])
-        order = [(0, 1), (1, 1), (0, 0), (1, 0)] if x_first(k) else [(1, 0), (1, 1), (0, 0), (0, 1)]
-        for n, (yy, xx) in enumerate(order):
+
+    def stage1(k, slot):
+        for other in (1, 0):
+            yy, xx = (slot, other) if x_first(k) else (other, slot)
             add(k, yy, xx, take.at[k, yy, xx])
-            if n < 2:
-                slot = yy if x_first(k) else xx
+            if other:
                 send(
                     mine.at[k, yy, xx], in1.at[k, slot], s1_send.at[k, slot], s1_recv.at[k, slot],
                     peer_x if x_first(k) else peer_y,
                 )
 
-    def stage2(k):
-        for slot in (1, 0):
-            arrived(in1.at[k, slot], s1_recv.at[k, slot])
-            yy, xx = (slot, 0) if x_first(k) else (0, slot)
-            add(k, yy, xx, in1.at[k, slot])
-            if slot:
-                send(mine.at[k, yy, xx], in2.at[k], s2_send.at[k], s2_recv.at[k], peer_y if x_first(k) else peer_x)
+    def stage2(k, slot):
+        arrived(in1.at[k, slot], s1_recv.at[k, slot])
+        yy, xx = (slot, 0) if x_first(k) else (0, slot)
+        add(k, yy, xx, in1.at[k, slot])
+        if slot:
+            send(mine.at[k, yy, xx], in2.at[k], s2_send.at[k], s2_recv.at[k], peer_y if x_first(k) else peer_x)
 
     def stage3(k):
         arrived(in2.at[k], s2_recv.at[k])
         add(k, 0, 0, in2.at[k])
         send(mine.at[k, 0, 0], in3.at[k], s3_send.at[k], s3_recv.at[k], peer_z[k])
 
-    def from_z(k):
-        got(0, 0, k, 0)
-        for axis in (1, 2, 0):
-            w_fwd(axis, 0, k, 0)
-
-    def diag_by_x(k):
-        return k == 0 or k == n_z - 1
-
-    def from_x(k):
-        got(1, 0, k, 0)
-        if not diag_by_x(k):
-            w_fwd(2, 1, k, 0)
-        w_fwd(0, 1, k, 0)
-
-    def from_y(k):
-        got(0, 0, k, 1)
-        if diag_by_x(k):
-            w_fwd(1, 0, k, 1)
-        w_fwd(0, 0, k, 1)
-
-    wfull[row_at(0, 0), :] = w_ref[...]
-    far = list(range(n_z - 1, -1, -1))
-    near = list(range(1, n_z))
-    partial(far[0])
-    from_y(0)
-    for n, k in enumerate(near):
-        partial(far[n + 1])
-        from_z(k)
-        stage1(far[n])
-    stage1(far[-1])
-    for n, k in enumerate(near):
-        from_x(k)
-        from_y(k)
-        stage2(far[n])
-    stage2(far[-1])
-    for k in range(n_z):
-        got(1, 0, k, 1)
-        w_fwd(0, 1, k, 1)
-    for k in far[:-1]:
-        stage3(k)
+    def take_on(xx, k, yy, *axes):
+        got(xx, 0, k, yy)
+        for axis in axes + (0,):
+            w_fwd(axis, xx, k, yy)
+
+    loads[2].wait()
+    partial(3)
+    take_on(0, 1, 0, 2)
+    partial(2)
+    core_in(3)
+    stage1(3, 1)
+    stage1(3, 0)
+    take_on(0, 2, 0, 2)
+    core_in(2)
+    stage1(2, 1)
+    stage1(2, 0)
+    take_on(0, 0, 1)
+    take_on(0, 1, 1, 1)
+    partial(1)
+    partial(0)
+    take_on(0, 2, 1, 1)
+    stage2(3, 1)
+    take_on(0, 3, 0, 1, 2)
+    core_in(1)
+    core_in(0)
+    stage2(3, 0)
+    take_on(1, 0, 1)
+    take_on(1, 1, 0)
+    stage2(2, 1)
+    take_on(1, 1, 1)
+    stage1(1, 1)
+    stage1(0, 1)
+    stage1(0, 0)
+    take_on(1, 2, 1)
+    take_on(0, 3, 1, 1)
+    stage1(1, 0)
+    take_on(1, 2, 0)
+    stage2(2, 0)
+    take_on(1, 3, 0)
+    stage3(3)
+    stage3(2)
+    stage2(1, 1)
+    stage2(0, 1)
+    take_on(1, 3, 1)
+    loads[3].wait()
     for k in range(n_z):
         for yy in (0, 1):
             for xx in (0, 1):
@@ -194,9 +218,12 @@
         dn[:, at] = d
         dt = d * tok_ref[:, at].astype(jnp.float32)
         gsend[0, :, at] = jnp.sum(dt * inv, axis=0, keepdims=True)
-        scaled = dt * gain_ref[:, at]
+        scaled = dt * gain_ref[at].reshape(1, -1)
         inner = inner + scaled[:, :LANES] + scaled[:, LANES:]
     send(gsend.at[0], grecv.at[0], g_send.at[0], g_recv.at[0], peer_c)
+    for k in (1, 0):
+        stage2(k, 0)
+    stage3(1)
     mean = jnp.sum(inner, axis=1, keepdims=True) / features
     pull = inv * inv * mean
 
@@ -204,7 +231,7 @@
         for j in range(lo, hi):
             at = slice(j * wide, (j + 1) * wide)
             t = tok_ref[:, at].astype(jnp.float32)
-            tg_ref[:, at] = (inv * (dn[:, at] * gain_ref[:, at] - t * pull)).astype(jnp.bfloat16)
+            tg_ref[:, at] = (inv * (dn[:, at] * gain_ref[at].reshape(1, -1) - t * pull)).astype(jnp.bfloat16)
 
     steps = features // wide
     cuts = [steps * n // 3 for n in range(4)]
@@ -231,7 +258,10 @@
         terms.append(grecv[2 + k])
     while len(terms) > 1:
         terms = [terms[i] + terms[i + 1] for i in range(0, len(terms), 2)]
-    gg_ref[...] = terms[0] * grad_scale
+    total = terms[0] * grad_scale
+    for j in range(features // LANES):
+        at = slice(j * LANES, (j + 1) * LANES)
+        gg_ref[at] = total[:, at].reshape(LANES)
     for copy in sends:
         copy.wait_send()
 
@@ -249,11 +279,15 @@
         out_shape=(
             jax.ShapeDtypeStruct((n_tok, features), bf16),
             jax.ShapeDtypeStruct(block, f32),
-            jax.ShapeDtypeStruct((1, features), f32),
+            jax.ShapeDtypeStruct((features,), f32),
         ),
-        in_specs=[vmem] * 4,
+        in_specs=[pl.BlockSpec(memory_space=pl.ANY)] * 4,
         out_specs=(vmem,) * 3,
         scratch_shapes=[
+            pltpu.VMEM((n_tok, features), bf16),
+            pltpu.VMEM((features,), f32),
+            pltpu.VMEM((n_tok, keys), bf16),
+            dma((4,)),
             pltpu.VMEM((features, keys), bf16),
             pltpu.VMEM((features, n_tok), bf16),
             pltpu.VMEM((n_tok, features), f32),
@@ -273,10 +307,10 @@
             dma((n_z + 2,)), dma((n_z + 2,)),
         ],
         compiler_params=pltpu.CompilerParams(
-            collective_id=0, has_side_effects=True, vmem_limit_bytes=48 * 1024 * 1024
+            collective_id=0, has_side_effects=True, vmem_limit_bytes=60 * 1024 * 1024
         ),
-    )(tokens, norm_gain.reshape(1, features), key_weight, key_grad)
-    return token_grad, weight_grad, gain_grad.reshape(features)
+    )(tokens, norm_gain, key_weight, key_grad)
+    return token_grad, weight_grad, gain_grad
 
 
 def plain(tokens, norm_gain, key_weight, key_grad):
@@ -312,7 +346,7 @@
     n_rep, n_grp = lax.axis_size("rep"), lax.axis_size("grp")
     n_z = n_grp // 2
     if (
-        n_rep == 2 * 2 and n_grp % 2 == 0 and n_z & (n_z - 1) == 0 and 1 < n_z <= 4
+        n_rep == 2 * 2 and n_grp == 2 * 4
         and key_weight.shape[1] % (n_rep * LANES) == 0 and key_weight.shape[0] % 16 == 0
         and tokens.shape[1] % (2 * LANES) == 0 and tokens.shape[0] % LANES == 0
     ):

time: 68 us -> 61.2 us (0.900)
  Pallas kernels: 60.6 us -> 56.7 us
  local copies, waits for them, and re-layouts: 5.81 us -> 3.72 us
    pallas_call x1, Pallas kernels: 60.6 us -> 56.7 us  [fused(): pl.pallas_call(functools.partial(kernel, n_z, grad_scale), out_shape=(jax...]
    unnamed x8 -> x7, local copies, waits for them, and re-layouts: 5.1 us -> 3.72 us
    reshape x1 -> x0, local copies, waits for them, and re-layouts: 0.71 us -> none  [fused(): norm_gain.reshape(1, features)]
where the time goes in v2:
time: 61.2 us; the launch traced here: 61.1 us
  Pallas kernels  56.7 us (93%)
  local copies, waits for them, and re-layouts  3.72 us (6%)
  between operations  0.66 us (1%)
    pallas_call x1, Pallas kernels, fused(): pl.pallas_call(functools.partial(kernel, n_z, grad_scale), out_shape=(jax...  56.7 us
    unnamed x7, local copies, waits for them, and re-layouts  3.72 us

profile of v2, /device:TPU:0, one launch (start us, length us, event | category | flops | bytes accessed | tf_op | source)
XLA Modules:
  0.0 61.1 jit_solution(13198229881870201588)
XLA Ops:
  0.6 56.7 %shard_map.67 = (bf16[256,2304]{1,0:T(8,128)(2,1)}, f32[288,256]{1,0:T(8,128)}, f32[2304]{0:T(1024)}) custom-call(bf16[256,2304]{1,0:T(8,128)(2,1)} %tok_hbm.1, f32[2304]{0:T(1024)} %gain_hbm.1, bf16[288,1024]{1,0:T(8,128)(2,1)} %w_ref.1, bf16[256,1024]{1,0:T(8,128)(2,1)} %kg_hbm.1), custom_call_target="tpu_custom_call" | custom-call | tf_op jit(solution)/shard_map/pallas_call | solution.py:277
  57.4 0.0 copy-start
  57.4 0.0 copy-start.1
  57.4 2.4 %copy.10 = bf16[256,2304]{1,0:T(8,128)(2,1)} copy(bf16[256,2304]{1,0:T(8,128)(2,1)} %get-tuple-element.6) | data formatting | bytes 2359296
  59.8 0.0 copy-done
  59.8 0.7 %copy.11 = f32[288,256]{1,0:T(8,128)} copy(f32[288,256]{1,0:T(8,128)S(1)} %copy-done) | data formatting | bytes 589824
  60.5 0.0 copy-done.1
  60.5 0.6 copy.12
Async XLA Ops:
  57.4 2.4 %copy-start = (f32[288,256]{1,0:T(8,128)S(1)}, f32[288,256]{1,0:T(8,128)}, u32[]{:S(2)}) copy-start(f32[288,256]{1,0:T(8,128)} %get-tuple-element.7) | copy-start | bytes 884740
  57.4 3.1 %copy-start.1 = (f32[2304]{0:T(1024)S(1)}, f32[2304]{0:T(1024)}, u32[]{:S(2)}) copy-start(f32[2304]{0:T(1024)} %get-tuple-element.8) | copy-start | bytes 27652

commit v3 on v2

--- a/solution.py
+++ b/solution.py
@@ -36,8 +36,12 @@
     cols = mine.shape[-1]
     peer_c = (2 * x + 1 - c, grp)
     peer_x = (2 * (1 - x) + c, grp)
+    peer_cx = (2 * (1 - x) + 1 - c, grp)
     peer_y = (rep, 2 * z + 1 - y)
     peer_z = [None] + [(rep, 2 * flip(z, k) + y) for k in range(1, n_z)]
+    group = [peer_y]
+    for k in range(1, n_z):
+        group += [peer_z[k], (rep, 2 * flip(z, k) + 1 - y)]
 
     def row_at(k, yy):
         g = 2 * flip(z, k) + (1 - y if yy else y)
@@ -53,7 +57,7 @@
         load.start()
 
     barrier = pltpu.get_barrier_semaphore()
-    peers = [peer_c, peer_x, peer_y] + peer_z[1:]
+    peers = [peer_c, peer_x, peer_cx] + group
     for peer in peers:
         pl.semaphore_signal(barrier, inc=1, device_id=peer, device_id_type=MESH)
     pl.semaphore_wait(barrier, len(peers))
@@ -220,7 +224,8 @@
         gsend[0, :, at] = jnp.sum(dt * inv, axis=0, keepdims=True)
         scaled = dt * gain_ref[at].reshape(1, -1)
         inner = inner + scaled[:, :LANES] + scaled[:, LANES:]
-    send(gsend.at[0], grecv.at[0], g_send.at[0], g_recv.at[0], peer_c)
+    for n, peer in enumerate((peer_c, peer_x, peer_cx)):
+        send(gsend.at[0], grecv.at[n], g_send.at[n], g_recv.at[n], peer)
     for k in (1, 0):
         stage2(k, 0)
     stage3(1)
@@ -234,16 +239,13 @@
             tg_ref[:, at] = (inv * (dn[:, at] * gain_ref[at].reshape(1, -1) - t * pull)).astype(jnp.bfloat16)
 
     steps = features // wide
-    cuts = [steps * n // 3 for n in range(4)]
-    for n, peer in enumerate((peer_x, peer_y, None)):
-        token_grad(cuts[n], cuts[n + 1])
+    token_grad(0, steps // 3)
+    for n in range(3):
         arrived(grecv.at[n], g_recv.at[n])
-        gsend[n + 1] = gsend[n] + grecv[n]
-        if peer is not None:
-            send(gsend.at[n + 1], grecv.at[n + 1], g_send.at[n + 1], g_recv.at[n + 1], peer)
-        else:
-            for k in range(1, n_z):
-                send(gsend.at[n + 1], grecv.at[2 + k], g_send.at[2 + k], g_recv.at[2 + k], peer_z[k])
+    gsend[1] = (gsend[0] + grecv[0]) + (grecv[1] + grecv[2])
+    for n, peer in enumerate(group):
+        send(gsend.at[1], grecv.at[3 + n], g_send.at[3 + n], g_recv.at[3 + n], peer)
+    token_grad(steps // 3, steps)
 
     arrived(in2.at[0], s2_recv.at[0])
     total = mine[0, 0, 0].astype(jnp.float32) + in2[0].astype(jnp.float32)
@@ -252,10 +254,10 @@
         total = total + in3[k].astype(jnp.float32)
     wg_ref[...] = total * grad_scale
 
-    terms = [gsend[3]]
-    for k in range(1, n_z):
-        arrived(grecv.at[2 + k], g_recv.at[2 + k])
-        terms.append(grecv[2 + k])
+    terms = [gsend[1]]
+    for n in range(3, 3 + len(group)):
+        arrived(grecv.at[n], g_recv.at[n])
+        terms.append(grecv[n])
     while len(terms) > 1:
         terms = [terms[i] + terms[i + 1] for i in range(0, len(terms), 2)]
     total = terms[0] * grad_scale
@@ -297,14 +299,14 @@
             pltpu.VMEM((n_z, 2) + block, bf16),
             pltpu.VMEM((n_z,) + block, bf16),
             pltpu.VMEM((n_z,) + block, bf16),
-            pltpu.VMEM((4, 1, features), f32),
-            pltpu.VMEM((n_z + 2, 1, features), f32),
+            pltpu.VMEM((2, 1, features), f32),
+            pltpu.VMEM((2 * n_z + 2, 1, features), f32),
             dma((4, 2, n_z, 2)), dma((2, 2, n_z, 2)),
             dma((n_z,)), dma((n_z,)),
             dma((n_z, 2)), dma((n_z, 2)),
             dma((n_z,)), dma((n_z,)),
             dma((n_z,)), dma((n_z,)),
-            dma((n_z + 2,)), dma((n_z + 2,)),
+            dma((2 * n_z + 2,)), dma((2 * n_z + 2,)),
         ],
         compiler_params=pltpu.CompilerParams(
             collective_id=0, has_side_effects=True, vmem_limit_bytes=60 * 1024 * 1024

time: 61.2 us -> 59.9 us (0.979)
  Pallas kernels: 56.7 us -> 55.4 us
    pallas_call x1, Pallas kernels: 56.7 us -> 55.4 us  [fused(): pl.pallas_call(functools.partial(kernel, n_z, grad_scale), out_shape=(jax...]
where the time goes in v3:
time: 59.9 us; the launch traced here: 59.8 us
  Pallas kernels  55.4 us (92%)
  local copies, waits for them, and re-layouts  3.72 us (6%)
  between operations  0.66 us (1%)
    pallas_call x1, Pallas kernels, fused(): pl.pallas_call(functools.partial(kernel, n_z, grad_scale), out_shape=(jax...  55.4 us
    unnamed x7, local copies, waits for them, and re-layouts  3.72 us

profile of v3, /device:TPU:0, one launch (start us, length us, event | category | flops | bytes accessed | tf_op | source)
XLA Modules:
  0.0 59.8 jit_solution(8925108120913528559)
XLA Ops:
  0.6 55.4 %shard_map.67 = (bf16[256,2304]{1,0:T(8,128)(2,1)}, f32[288,256]{1,0:T(8,128)}, f32[2304]{0:T(1024)}) custom-call(bf16[256,2304]{1,0:T(8,128)(2,1)} %tok_hbm.1, f32[2304]{0:T(1024)} %gain_hbm.1, bf16[288,1024]{1,0:T(8,128)(2,1)} %w_ref.1, bf16[256,1024]{1,0:T(8,128)(2,1)} %kg_hbm.1), custom_call_target="tpu_custom_call" | custom-call | tf_op jit(solution)/shard_map/pallas_call | solution.py:279
  56.0 0.0 copy-start
  56.0 0.0 copy-start.1
  56.0 2.4 %copy.10 = bf16[256,2304]{1,0:T(8,128)(2,1)} copy(bf16[256,2304]{1,0:T(8,128)(2,1)} %get-tuple-element.6) | data formatting | bytes 2359296
  58.4 0.0 copy-done
  58.4 0.7 %copy.11 = f32[288,256]{1,0:T(8,128)} copy(f32[288,256]{1,0:T(8,128)S(1)} %copy-done) | data formatting | bytes 589824
  59.2 0.0 copy-done.1
  59.2 0.6 %copy.12 = f32[2304]{0:T(1024)} copy(f32[2304]{0:T(1024)S(1)} %copy-done.1) | data formatting | bytes 18432
Async XLA Ops:
  56.0 2.4 %copy-start = (f32[288,256]{1,0:T(8,128)S(1)}, f32[288,256]{1,0:T(8,128)}, u32[]{:S(2)}) copy-start(f32[288,256]{1,0:T(8,128)} %get-tuple-element.7) | copy-start | bytes 884740
  56.0 3.1 %copy-start.1 = (f32[2304]{0:T(1024)S(1)}, f32[2304]{0:T(1024)}, u32[]{:S(2)}) copy-start(f32[2304]{0:T(1024)} %get-tuple-element.8) | copy-start | bytes 27652
